TPU v7x, 32 devices: a whole 2x2x4 slice. The times are simulated.
32 devices in a mesh: dp: 4 (over y, x), expert: 8 (over z, core).
Axes of the slice: x: 2, y: 2, z: 4, core: 2. Of those that a mesh axis runs over, the one named last changes fastest.
Arguments:
- expert_ids: int32 [1024, 4], P(('dp', 'expert')), may hold values from 0 to 7, all different within a row; in each aligned block of 32 rows (0 to 31, 32 to 63, ...) at most 20 rows name the same one
- expert_home: int32 [8], replicated, may hold values from 0 to 7, each once
- live_tokens: int32 [32], P(('dp', 'expert')), may hold values from 1 to 32, 768 in all
- gate_weights: float32 [1024, 4], P(('dp', 'expert')), may hold values from 0.1 to 1
- output_grad: bfloat16 [1024, 7168], P(('dp', 'expert')), may hold values from -6 to 6
- saved_hidden: bfloat16 [1024, 4, 1024], P(('dp', 'expert')), may hold values from -0.59765625 to 0.59765625
- down_weight: bfloat16 [8, 1024, 7168], P('expert'), may hold values from -0.1875 to 0.1875
- dense_input: bfloat16 [1024, 7168], P(('dp', 'expert')), may hold values from -6 to 6
- latent_grad: bfloat16 [1024, 256], P(('dp', 'expert')), may hold values from -0.1875 to 0.1875
Outputs:
- hidden_grad: bfloat16 [1024, 4, 1024], P(('dp', 'expert'))
- expert_grad: float32 [8, 1024, 7168], P('expert', 'dp')
- dense_grad: float32 [7168, 256], P(('dp', 'expert'))
Inputs may be any that keep to these rules, and one draw needn't show every extreme that they name: `expert_ids`: each row names 4 different experts. Among the rows of one device no expert is named more than 20 times, and on some devices one expert is named exactly 20 times. A permutation: expert e is held at index expert_home[e] of the expert axis, in every dp replica. `live_tokens`: entry i is the number of real tokens at the start of device i, in the order of the joined dp and expert axes; the rest are padding. Some device has all 32 real.
All inputs are finite; a program needn't handle non-finite values.
Results may differ from a plain program's by a relative error of at most 0.008.
Values may be sent and summed in bfloat16 or wider, within the bound.
No kernel may reach another device: no remote copies, remote signals or barrier semaphores. Data moves between devices by JAX's collectives and lax.ppermute only.
A program may use at most 192 MiB of HBM per device.

v0:
```python
import jax
import jax.numpy as jnp
from jax import lax
from jax.sharding import PartitionSpec as P


def on_device(
    expert_ids,
    expert_home,
    live_tokens,
    gate_weights,
    output_grad,
    saved_hidden,
    down_weight,
    dense_input,
    latent_grad,
):
    n_group = lax.axis_size("expert")
    tok_rows, top_count = expert_ids.shape
    model_width = output_grad.shape[1]
    hidden_units = saved_hidden.shape[2]
    capacity = tok_rows * top_count * 5 // (4 * n_group)
    is_live = jnp.arange(tok_rows, dtype=jnp.int32) < live_tokens[0]
    masked_grad = jnp.where(is_live[:, None], latent_grad, jnp.zeros_like(latent_grad))
    owned_columns = lax.all_to_all(
        dense_input, ("dp", "expert"), split_axis=1, concat_axis=0, tiled=True
    )
    dense_grad = lax.dot_general(
        owned_columns,
        lax.all_gather(masked_grad, ("dp", "expert"), axis=0, tiled=True),
        (((0,), (0,)), ((), ())),
        preferred_element_type=jnp.float32,
    )
    pair_count = tok_rows * top_count
    flat_ids = expert_ids.reshape(pair_count)
    expert_count = expert_home.shape[0]
    id_table = (flat_ids[:, None] == jnp.arange(expert_count, dtype=jnp.int32)[None, :]).astype(
        jnp.int32
    )
    home_slot = jnp.sum(id_table * expert_home[None, :], axis=1)
    slot_table = (home_slot[:, None] == jnp.arange(n_group, dtype=jnp.int32)[None, :]).astype(
        jnp.int32
    )
    earlier = jnp.cumsum(slot_table, axis=0) - slot_table
    position = jnp.sum(earlier * slot_table, axis=1)
    slot_index = home_slot * capacity + position
    pair_ids = jnp.arange(pair_count, dtype=jnp.int32)
    source_pair = jnp.zeros((n_group * capacity,), jnp.int32).at[slot_index].set(pair_ids)
    filled = jnp.zeros((n_group * capacity,), jnp.bool_).at[slot_index].set(True)
    source_token = source_pair // top_count
    pair_scale = (gate_weights * is_live[:, None].astype(jnp.float32)).reshape(pair_count)
    slot_scale = jnp.where(filled, pair_scale[source_pair], jnp.float32(0.0))
    grad_rows = (output_grad[source_token].astype(jnp.float32) * slot_scale[:, None]).astype(
        jnp.bfloat16
    )
    flat_hidden = saved_hidden.reshape(pair_count, hidden_units)
    hidden_rows = jnp.where(filled[:, None], flat_hidden[source_pair], jnp.zeros((), jnp.bfloat16))
    arrived_grad, arrived_hidden = (
        lax.all_to_all(
            grad_rows.reshape(n_group, capacity, model_width),
            "expert",
            split_axis=0,
            concat_axis=0,
            tiled=True,
        ),
        lax.all_to_all(
            hidden_rows.reshape(n_group, capacity, hidden_units),
            "expert",
            split_axis=0,
            concat_axis=0,
            tiled=True,
        ),
    )
    arrived_grad = arrived_grad.reshape(n_group * capacity, model_width)
    arrived_hidden = arrived_hidden.reshape(n_group * capacity, hidden_units)
    expert_weight = down_weight[0]
    input_grad = lax.dot_general(
        arrived_grad, expert_weight, (((1,), (1,)), ((), ())), preferred_element_type=jnp.float32
    ).astype(jnp.bfloat16)
    returned = lax.all_to_all(
        input_grad.reshape(n_group, capacity, hidden_units),
        "expert",
        split_axis=0,
        concat_axis=0,
        tiled=True,
    )
    expert_grad = lax.psum_scatter(
        lax.dot_general(
            arrived_hidden,
            arrived_grad,
            (((0,), (0,)), ((), ())),
            preferred_element_type=jnp.float32,
        ),
        "dp",
        scatter_dimension=0,
        tiled=True,
    )
    hidden_grad = returned.reshape(n_group * capacity, hidden_units)[slot_index].reshape(
        tok_rows, top_count, hidden_units
    )
    return (hidden_grad, expert_grad[None], dense_grad)


def solution(mesh):
    placed = (
        P(("dp", "expert"), None),
        P(),
        P(("dp", "expert")),
        P(("dp", "expert"), None),
        P(("dp", "expert"), None),
        P(("dp", "expert"), None, None),
        P("expert", None, None),
        P(("dp", "expert"), None),
        P(("dp", "expert"), None),
    )
    return jax.shard_map(
        on_device,
        mesh=mesh,
        in_specs=placed,
        out_specs=(
            P(("dp", "expert"), None, None),
            P("expert", "dp", None),
            P(("dp", "expert"), None),
        ),
        check_vma=False,
    )
```

profile of v0, /device:TPU:0, one launch (start us, length us, event | category | flops | bytes accessed | tf_op | source)
XLA Modules:
  0.0 383.3 jit_solution(13463174959926582914)
XLA Ops:
  7.2 0.0 copy-start
  7.2 0.8 copy.14
  8.0 0.1 eq.28
  8.1 0.8 select_reduce_fusion.1
  8.9 0.1 fusion.5
  9.0 0.2 reduce_window_sum.11
  9.2 0.2 select_reduce_fusion
  9.4 1.0 scatter_custom_fusion
  10.4 1.0 reshape.88
  11.4 0.9 gather_fusion.3
  12.4 0.1 gather.18
  12.5 1.0 scatter_custom_fusion.1
  13.5 0.1 broadcast_in_dim.61
  13.6 0.9 broadcast_select_fusion
  14.4 6.4 %all-to-all-start.2 = ((bf16[8,20,1024]{2,1,0:T(8,128)(2,1)}), bf16[8,20,1024]{2,1,0:T(8,128)(2,1)}, u32[]{:S(2)}, u32[]{:S(2)}) async-start(bf16[8,20,1024]{2,1,0:T(8,128)(2,1)} %broadcast_select_fusion), calls=%async_computation.2 | async-start | bytes 786432 | tf_op jit(solution)/shard_map/all_to_all | solution.py:66
  20.8 0.0 reduce-scatter.2.cloned.1.call-start
  20.8 0.0 copy-done
  20.8 2.0 gather_fusion
  22.9 0.0 copy-start.6
  22.9 2.9 reshape.89
  26.4 0.0 copy-done.6
  26.4 0.1 copy.15
  26.5 0.1 reshape.83
  26.6 1.6 gather_fusion.1
  28.2 0.1 mul.51
  28.3 3.1 multiply_convert_fusion
  31.4 2.1 all-to-all-done.2
  33.4 65.9 %all_to_all.34 = bf16[8,20,7168]{2,1,0:T(8,128)(2,1)S(1)} all-to-all(bf16[8,20,7168]{2,1,0:T(8,128)(2,1)S(1)} %multiply_convert_fusion), channel_id=1, replica_groups=mesh['dp'=4,'expert'=8] {'expert'}, dimensions={0} | all-to-all | bytes 4587520 | tf_op jit(solution)/shard_map/all_to_all | solution.py:59
  99.3 0.0 copy-start.2
  99.3 1.5 copy-done.2
  100.8 12.7 %convolution_bitcast_fusion = f32[1024,7168]{1,0:T(8,128)} fusion(bf16[8,20,1024]{2,1,0:T(8,128)(2,1)} %all-to-all-done.2, bf16[8,20,7168]{2,1,0:T(8,128)(2,1)S(1)} %all_to_all.34), kind=kOutput, calls=%fused_computation.6 | convolution fusion | flops 2348810240 | bytes 31981568 | tf_op jit(solution)/shard_map/dot_general | solution.py:88
  113.5 0.0 copy-start.4
  113.5 0.0 reduce-scatter.2.cloned.1.call-update
  113.5 1.0 copy-done.4
  114.5 0.0 copy-start.5
  114.5 0.0 copy-start.3
  114.5 1.6 all_to_all.26
  116.1 2.1 copy.16
  118.2 3.7 all-to-all-start.3
  121.9 0.0 copy-done.5
  121.9 0.1 broadcast_select_fusion.1
  122.0 0.0 copy-done.3
  122.0 2.1 reshape.84
  124.2 10.9 %fusion.2 = bf16[160,1024]{1,0:T(8,128)(2,1)S(1)} fusion(bf16[160,7168]{1,0:T(8,128)(2,1)} %reshape.84, bf16[1,1024,7168]{2,1,0:T(8,128)(2,1)} %param.15), kind=kOutput, calls=%fused_computation.10 | convolution fusion | flops 2348974080 | bytes 17301504 | tf_op jit(solution)/shard_map/dot_general | solution.py:77
  135.0 0.8 reshape.85
  135.9 2.4 all-to-all-done.3
  138.2 3.5 all-to-all-start.1
  141.7 0.0 copy-start.1
  141.7 45.2 %all_gather.3 = bf16[1024,256]{1,0:T(8,128)(2,1)S(1)} all-gather(bf16[32,256]{1,0:T(8,128)(2,1)S(1)} %broadcast_select_fusion.1), channel_id=1, replica_groups=mesh['dp'=4,'expert'=8] {'dp','expert'}, dimensions={0}, use_global_device_ids=true | all-gather | bytes 540672 | tf_op jit(solution)/shard_map/all_gather | solution.py:30
  186.9 2.1 convolution_bitcast_fusion.1
  189.0 0.0 all-to-all-done.1
  189.0 0.1 reshape.86
  189.1 0.9 gather_fusion.2
  189.9 0.8 reshape.87
  190.7 185.7 %reduce-scatter.2.cloned.1.call-done = f32[256,7168]{1,0:T(8,128)} async-done(((f32[1024,7168]{1,0:T(8,128)}), f32[256,7168]{1,0:T(8,128)}) %reduce-scatter.2.cloned.1.call-update) | async-done | bytes 7340048 | tf_op jit(solution)/shard_map/reduce_scatter | solution.py:87
  376.4 0.0 copy-done.1
  (10 shorter events, 0.1 us)
Async XLA Ops:
  7.2 13.7 %copy-start = (bf16[32,7168]{1,0:T(8,128)(2,1)S(1)}, bf16[32,7168]{1,0:T(8,128)(2,1)}, u32[]{:S(2)}) copy-start(bf16[32,7168]{1,0:T(8,128)(2,1)} %param.13) | copy-start | bytes 1376260
  14.4 19.0 %all-to-all-start.2 = ((bf16[8,20,1024]{2,1,0:T(8,128)(2,1)}), bf16[8,20,1024]{2,1,0:T(8,128)(2,1)}, u32[]{:S(2)}, u32[]{:S(2)}) async-start(bf16[8,20,1024]{2,1,0:T(8,128)(2,1)} %broadcast_select_fusion), calls=%async_computation.2 | async-start | bytes 786432 | tf_op jit(solution)/shard_map/all_to_all | solution.py:66
  20.8 355.6 %reduce-scatter.2.cloned.1.call-start = ((), (), s32[]{:S(2)}) async-start(), calls=%async_computation.5 | async-start | bytes 36700160 | tf_op jit(solution)/shard_map/reduce_scatter | solution.py:87
  22.9 3.6 copy-start.6
  99.3 1.5 copy-start.2
  113.5 1.0 copy-start.4
  114.5 7.4 %copy-start.5 = (bf16[32,256]{1,0:T(8,128)(2,1)S(1)}, bf16[32,256]{1,0:T(8,128)(2,1)}, u32[]{:S(2)}) copy-start(bf16[32,256]{1,0:T(8,128)(2,1)} %param.17) | copy-start | bytes 49156
  114.5 7.5 %copy-start.3 = (bf16[8,20,7168]{2,1,0:T(8,128)(2,1)S(1)}, bf16[8,20,7168]{2,1,0:T(8,128)(2,1)}, u32[]{:S(2)}) copy-start(bf16[8,20,7168]{2,1,0:T(8,128)(2,1)} %copy-done.2) | copy-start | bytes 6881284
  118.2 20.0 %all-to-all-start.3 = ((bf16[32,32,224]{2,0,1:T(8,128)(2,1)}), bf16[32,32,224]{2,0,1:T(8,128)(2,1)}, u32[]{:S(2)}, u32[]{:S(2)}) async-start(bf16[32,32,224]{2,0,1:T(8,128)(2,1)} %copy.16), calls=%async_computation.4 | async-start | bytes 1048576 | tf_op jit(solution)/shard_map/all_to_all | solution.py:25
  138.2 50.7 %all-to-all-start.1 = ((bf16[8,20,1024]{2,1,0:T(8,128)(2,1)}), bf16[8,20,1024]{2,1,0:T(8,128)(2,1)S(1)}, u32[]{:S(2)}, u32[]{:S(2)}) async-start(bf16[8,20,1024]{2,1,0:T(8,128)(2,1)} %reshape.85), calls=%async_computation.1 | async-start | bytes 786432 | tf_op jit(solution)/shard_map/all_to_all | solution.py:80
  141.7 234.7 %copy-start.1 = (bf16[32,7168]{1,0:T(8,128)(2,1)S(1)}, bf16[32,7168]{1,0:T(8,128)(2,1)}, u32[]{:S(2)}) copy-start(bf16[32,7168]{1,0:T(8,128)(2,1)} %param.13) | copy-start | bytes 1376260
Sparse Core Ops, SparseCore 0:
  113.7 262.6 reduce-scatter.1
where the time goes:
time: 384 us; the launch traced here: 383 us
  waiting for transfers between devices  190 us (49%)
  blocking collectives  111 us (29%)
  matrix products  25.6 us (7%)
  local copies, waits for them, and re-layouts  22.7 us (6%)
  between operations  14.9 us (4%)
  starting transfers between devices  13.5 us (4%)
  other arithmetic  5.34 us (1%)
    reduce_scatter x1, waiting for transfers between devices, on_device(): lax.psum_scatter(lax.dot_general(arrived_hidden, arrived_grad, (((0,), (0...  186 us
    all_to_all x1, blocking collectives, on_device(): lax.all_to_all(grad_rows.reshape(n_group, capacity, model_width), 'expert...  65.9 us
    all_gather x1, blocking collectives, on_device(): lax.all_gather(masked_grad, ('dp', 'expert'), axis=0, tiled=True)  45.2 us
    dot_general x1, matrix products, on_device(): lax.dot_general(arrived_hidden, arrived_grad, (((0,), (0,)), ((), ())), p...  12.7 us
    dot_general x1, matrix products, on_device(): lax.dot_general(arrived_grad, expert_weight, (((1,), (1,)), ((), ())), pr...  10.9 us
  transfers between devices with their start and end apart: 4, of which 3 were waited for; matrix products, arithmetic and copies ran while one was open for 8% of the time, Pallas kernels for 0%

commit v1 on v0

v1 whole, which is shorter than its diff:
```python
import jax
import jax.numpy as jnp
from jax import lax
from jax.sharding import PartitionSpec as P

ALL = ("dp", "expert")


class Torus:
    def __init__(self, n_dp, n_group):
        n_x = 2 if n_dp % 2 == 0 else 1
        self.n_core = 2
        self.shape = (n_dp // n_x, n_x, n_group // self.n_core)
        self.n_dev = n_dp * n_group
        self.n_group = n_group

    def coords(self, d):
        dp, e = divmod(d, self.n_group)
        y, x = divmod(dp, self.shape[1])
        z, core = divmod(e, self.n_core)
        return [y, x, z, core]

    def index(self, c):
        return ((c[0] * self.shape[1] + c[1]) * self.shape[2] + c[2]) * self.n_core + c[3]

    def fetch(self, piece, axis, step):
        rows, labels = piece
        size = self.shape[axis]
        pairs = []
        for d in range(self.n_dev):
            c = self.coords(d)
            c[axis] = (c[axis] - step) % size
            pairs.append((d, self.index(c)))
        moved = [
            tuple((v + step) % size if i == axis else v for i, v in enumerate(label))
            for label in labels
        ]
        return lax.ppermute(rows, ALL, pairs), moved

    def swap(self, rows):
        return lax.ppermute(rows, ALL, [(d, d ^ 1) for d in range(self.n_dev)])

    def others(self, piece, axis):
        size = self.shape[axis]
        found, up, down = [], piece, piece
        for _ in range((size - 1) // 2):
            up, down = self.fetch(up, axis, 1), self.fetch(down, axis, -1)
            found += [up, down]
        if size % 2 == 0 and size > 2:
            found += [self.fetch(halves(up)[0], axis, 1), self.fetch(halves(down)[1], axis, -1)]
        elif size == 2:
            found.append(self.fetch(piece, axis, 1))
        return found

    def across(self, piece):
        early, late = [], []
        for part, (first, second) in zip(halves(piece), ((1, 0), (0, 1))):
            near = self.others(part, first)
            late += self.others(joined([part] + near), second)
            early += near
        return early, late


def halves(piece):
    rows, labels = piece
    unit = rows.shape[0] // len(labels)
    cut = len(labels) // 2
    return (rows[: cut * unit], labels[:cut]), (rows[cut * unit :], labels[cut:])


def joined(pieces):
    return jnp.concatenate([p[0] for p in pieces], axis=0), sum([p[1] for p in pieces], [])


def on_device(
    expert_ids,
    expert_home,
    live_tokens,
    gate_weights,
    output_grad,
    saved_hidden,
    down_weight,
    dense_input,
    latent_grad,
):
    n_group = lax.axis_size("expert")
    n_dp = lax.axis_size("dp")
    n_dev = n_group * n_dp
    tok_rows, top_count = expert_ids.shape
    model_width = output_grad.shape[1]
    hidden_units = saved_hidden.shape[2]
    block_units = hidden_units // n_dp
    is_live = jnp.arange(tok_rows, dtype=jnp.int32) < live_tokens[0]
    masked_grad = jnp.where(is_live[:, None], latent_grad, jnp.zeros_like(latent_grad))
    torus = Torus(n_dp, n_group)
    n_core = torus.n_core
    n_y, n_x, n_z = torus.shape
    core = lax.axis_index("expert") % n_core
    place_z = lax.axis_index("expert") // n_core
    place_y = lax.axis_index("dp") // n_x
    place_x = lax.axis_index("dp") % n_x
    n_unit = 4
    unit = tok_rows // n_unit
    start = (output_grad, [(0, 0, 0, u) for u in range(n_unit)])
    near = joined([start] + torus.others(start, 2))
    id_table = expert_ids[:, :, None] == jnp.arange(expert_home.shape[0], dtype=jnp.int32)
    home_slot = jnp.sum(jnp.where(id_table, expert_home, 0), axis=2)
    pair_scale = gate_weights * is_live[:, None].astype(jnp.float32)
    chosen = home_slot[None] == jnp.arange(n_group, dtype=jnp.int32)[:, None, None]
    scaled = (saved_hidden.astype(jnp.float32) * pair_scale[:, :, None])
    spread = sum(
        jnp.where(chosen[:, :, k, None], scaled[None, :, k], jnp.float32(0.0))
        for k in range(top_count)
    ).astype(jnp.bfloat16)
    owned_width = model_width // n_dev
    latent_width = masked_grad.shape[1]
    outgoing = jnp.concatenate(
        [
            spread.reshape(n_group, tok_rows, n_dp, block_units)
            .transpose(2, 0, 1, 3)
            .reshape(n_dev, tok_rows, block_units),
            jnp.broadcast_to(masked_grad[None], (n_dev, tok_rows, latent_width)),
            dense_input.reshape(tok_rows, n_dev, owned_width).transpose(1, 0, 2),
        ],
        axis=2,
    )
    arrived = lax.all_to_all(outgoing, ALL, split_axis=0, concat_axis=0, tiled=True)
    ready, _ = lax.optimization_barrier((near[0], outgoing))
    near = (ready, near[1])
    a_rows = [(near[0][i * unit : (i + 1) * unit], [l]) for i, l in enumerate(near[1]) if l[3] < n_unit // 2]
    a_early, a_late = torus.across(joined(a_rows))
    b_early, b_late = torus.across(halves(start)[1])
    b_cross = joined(b_early + b_late)
    b_far = [b_cross] + torus.others(b_cross, 2)
    groups = [near, joined(a_early), joined(b_far), joined(a_late)]
    near_other = torus.swap(near[0])
    swapped = [near_other] + [torus.swap(g[0]) for g in groups[1:]]

    flat = arrived.reshape(n_dev * tok_rows, -1)
    dense_grad = lax.dot_general(
        flat[:, block_units + latent_width :],
        flat[:, block_units : block_units + latent_width],
        (((0,), (0,)), ((), ())),
        preferred_element_type=jnp.float32,
    )
    relative = arrived[..., :block_units].reshape(
        n_y, n_x, n_z, n_core, n_unit, unit, block_units
    )
    relative = jnp.roll(relative, -place_y, axis=0)
    relative = jnp.roll(relative, -place_x, axis=1)
    relative = jnp.roll(relative, -place_z, axis=2)
    relative = jnp.roll(relative, -core, axis=3)

    def hidden_of(labels, c):
        return jnp.concatenate([relative[y, x, z, c, u] for y, x, z, u in labels], axis=0)

    weight = down_weight[0]

    def through(rows):
        return lax.dot_general(
            rows, weight, (((1,), (1,)), ((), ())), preferred_element_type=jnp.float32
        ).astype(jnp.bfloat16)

    def in_order(rows):
        blocks = {l[2:]: rows[i * unit : (i + 1) * unit] for i, l in enumerate(near[1])}
        return jnp.stack(
            [
                jnp.concatenate([blocks[z, u] for u in range(n_unit)], axis=0)
                for z in range(n_z)
            ],
            axis=0,
        )

    part_mine = through(near[0])
    part_other = through(near_other)
    part_mine, part_other = in_order(part_mine), in_order(part_other)
    input_grad = jnp.roll(
        jnp.roll(jnp.stack([part_mine, part_other], axis=1), core, axis=1), place_z, axis=0
    )
    returned = lax.all_to_all(
        input_grad.reshape(n_group, tok_rows, hidden_units),
        "expert",
        split_axis=0,
        concat_axis=0,
        tiled=True,
    )
    over_tokens = (((0,), (0,)), ((), ()))

    def over_tokens(some):
        hidden = [hidden_of(groups[i][1], c) for c in range(n_core) for i in some]
        rows = [groups[i][0] for i in some] + [swapped[i] for i in some]
        return lax.dot_general(
            jnp.concatenate(hidden, axis=0),
            jnp.concatenate(rows, axis=0),
            (((0,), (0,)), ((), ())),
            preferred_element_type=jnp.float32,
        )

    near_sum = over_tokens([0])
    expert_grad = near_sum + over_tokens([1, 2, 3])
    picked = sum(
        jnp.where(chosen[s, :, :, None], returned[s][:, None, :].astype(jnp.float32), 0.0)
        for s in range(n_group)
    )
    hidden_grad = (picked * pair_scale[:, :, None]).astype(jnp.bfloat16)
    return (hidden_grad, expert_grad[None], dense_grad)


def solution(mesh):
    placed = (
        P(ALL, None),
        P(),
        P(ALL),
        P(ALL, None),
        P(ALL, None),
        P(ALL, None, None),
        P("expert", None, None),
        P(ALL, None),
        P(ALL, None),
    )
    return jax.shard_map(
        on_device,
        mesh=mesh,
        in_specs=placed,
        out_specs=(P(ALL, None, None), P("expert", "dp", None), P(ALL, None)),
        check_vma=False,
    )
```

time: 384 us -> 205 us (0.53)
  waiting for transfers between devices: 190 us -> 75.1 us
  blocking collectives: 111 us -> 0 us
  starting transfers between devices: 13.5 us -> 43.8 us
  local copies, waits for them, and re-layouts: 22.7 us -> 38.8 us
  between operations: 14.9 us -> 2.67 us
  matrix products: 25.6 us -> 32.1 us
  other arithmetic: 5.34 us -> 11.7 us
    reduce_scatter x1 -> x0, waiting for transfers between devices: 186 us -> none  [on_device(): lax.psum_scatter(lax.dot_general(arrived_hidden, arrived_grad, (((0,), (0...]
    all_to_all x1 -> x0, blocking collectives: 65.9 us -> none  [on_device(): lax.all_to_all(grad_rows.reshape(n_group, capacity, model_width), 'expert...]
    ppermute x0 -> x20, waiting for transfers between devices: none -> 64.2 us  [the longest x16 64.2 us: fetch(): return (lax.ppermute(rows, ALL, pairs), moved)]
    all_gather x1 -> x0, blocking collectives: 45.2 us -> none  [on_device(): lax.all_gather(masked_grad, ('dp', 'expert'), axis=0, tiled=True)]
    ppermute x0 -> x20, starting transfers between devices: none -> 33.6 us  [the longest x16 33.6 us: fetch(): return (lax.ppermute(rows, ALL, pairs), moved)]
    unnamed x15 -> x139, local copies, waits for them, and re-layouts: 3.38 us -> 20.3 us
    broadcast_in_dim x2 -> x20, local copies, waits for them, and re-layouts: 0.09 us -> 6.84 us  [the longest x8 6.41 us: on_device(): jnp.where(chosen[s, :, :, None], returned[s][:, None, :].astype(jnp.float...]
    all_to_all x3 -> x2, waiting for transfers between devices: 4.42 us -> 10.9 us  [the longest x1 10.9 us: on_device(): lax.all_to_all(input_grad.reshape(n_group, tok_rows, hidden_units), 'expe...]
  transfers between devices with their start and end apart: 4 -> 22, of which waited for: 3 -> 8; matrix products, arithmetic and copies ran while one was open for 8% -> 33% of each run, Pallas kernels for 0% -> 0%
where the time goes in v1:
time: 205 us; the launch traced here: 204 us
  waiting for transfers between devices  75.1 us (37%)
  starting transfers between devices  43.8 us (21%)
  local copies, waits for them, and re-layouts  38.8 us (19%)
  matrix products  32.1 us (16%)
  other arithmetic  11.7 us (6%)
  between operations  2.67 us (1%)
    ppermute x16, waiting for transfers between devices, fetch(): return (lax.ppermute(rows, ALL, pairs), moved)  64.2 us
    ppermute x16, starting transfers between devices, fetch(): return (lax.ppermute(rows, ALL, pairs), moved)  33.6 us
    dot_general x2, matrix products, through(): lax.dot_general(rows, weight, (((1,), (1,)), ((), ())), preferred_element...  20.9 us
    unnamed x139, local copies, waits for them, and re-layouts  20.3 us
    all_to_all x1, waiting for transfers between devices, on_device(): lax.all_to_all(input_grad.reshape(n_group, tok_rows, hidden_units), 'expe...  10.9 us
    dot_general x2, matrix products, over_tokens(): lax.dot_general(jnp.concatenate(hidden, axis=0), jnp.concatenate(rows, ax...  10.2 us
    broadcast_in_dim x8, local copies, waits for them, and re-layouts, on_device(): jnp.where(chosen[s, :, :, None], returned[s][:, None, :].astype(jnp.float...  6.41 us
    all_to_all x1, starting transfers between devices, on_device(): lax.all_to_all(outgoing, ALL, split_axis=0, concat_axis=0, tiled=True)  6.07 us
  transfers between devices with their start and end apart: 22, of which 8 were waited for; matrix products, arithmetic and copies ran while one was open for 33% of the time, Pallas kernels for 0%

profile of v1, /device:TPU:0, one launch (start us, length us, event | category | flops | bytes accessed | tf_op | source)
XLA Modules:
  0.0 204.3 jit_solution(6512106511568872518)
XLA Ops:
  0.6 5.1 %collective-permute-start = (bf16[32,7168]{1,0:T(8,128)(2,1)}, bf16[32,7168]{1,0:T(8,128)(2,1)}, u32[]{:S(2)}, u32[]{:S(2)}) collective-permute-start(bf16[32,7168]{1,0:T(8,128)(2,1)} %param.13), channel_id=1, source_target_pairs={{0,6},{1,7},{2,0},{3,1},{4,2},{5,3},{6,4},{7,5},{8,14},{9,15},{10,... | collective-permute-start | bytes 1376264 | tf_op jit(solution)/shard_map/ppermute | solution.py:38
  5.8 1.8 reshape.132
  8.5 0.7 broadcast_multiply_fusion
  9.3 1.1 convert_multiply_fusion
  10.4 1.4 slice_reduce_fusion.3
  12.4 0.7 fusion.15
  13.2 1.3 pad_maximum_fusion.1
  14.6 6.1 %all-to-all-start.1 = ((bf16[32,32,736]{2,1,0:T(8,128)(2,1)}), bf16[32,32,736]{2,1,0:T(8,128)(2,1)S(1)}, u32[]{:S(2)}, u32[]{:S(2)}) async-start(bf16[32,32,736]{2,1,0:T(8,128)(2,1)} %pad_maximum_fusion.1), calls=%async_computation.1 | async-start | bytes 3145728 | tf_op jit(solution)/shard_map/all_to_all | solution.py:127
  20.7 0.7 fusion.40
  21.4 1.8 collective-permute-start.7
  23.1 1.5 collective-permute-start.8
  24.6 1.0 constant_dynamic-update-slice_fusion.4
  26.7 0.7 copy.78
  27.4 1.4 copy.77
  28.7 1.3 copy.76
  30.1 1.3 copy.75
  31.4 1.4 copy.74
  32.8 1.0 pad_maximum_fusion.7
  33.8 0.8 collective-permute-start.9
  34.6 0.9 pad_maximum_fusion.8
  36.2 1.0 slice.740
  37.1 6.7 %collective-permute-start.2 = (bf16[16,7168]{1,0:T(8,128)(2,1)S(1)}, bf16[16,7168]{1,0:T(8,128)(2,1)S(1)}, u32[]{:S(2)}, u32[]{:S(2)}) collective-permute-start(bf16[16,7168]{1,0:T(8,128)(2,1)S(1)} %slice.740), channel_id=1, source_target_pairs={{0,6},{1,7},{2,0},{3,1},{4,2},{5,3},{6,4},{7,5},{8,14},{9,15},{10,... | collective-permute-start | bytes 688136 | tf_op jit(solution)/shard_map/ppermute | solution.py:38
  43.8 1.0 slice.741
  44.9 1.1 constant_dynamic-update-slice_fusion.3
  45.9 1.1 constant_dynamic-update-slice_fusion.2
  47.0 10.1 %collective-permute-done.2 = bf16[16,7168]{1,0:T(8,128)(2,1)S(1)} collective-permute-done((bf16[16,7168]{1,0:T(8,128)(2,1)S(1)}, bf16[16,7168]{1,0:T(8,128)(2,1)S(1)}, u32[]{:S(2)}, u32[]{:S(2)}) %collective-permute-start.2) | collective-permute-done | bytes 229408 | tf_op jit(solution)/shard_map/ppermute | solution.py:38
  57.1 4.7 %collective-permute-done.3 = bf16[16,7168]{1,0:T(8,128)(2,1)S(1)} collective-permute-done((bf16[16,7168]{1,0:T(8,128)(2,1)S(1)}, bf16[16,7168]{1,0:T(8,128)(2,1)S(1)}, u32[]{:S(2)}, u32[]{:S(2)}) %collective-permute-start.3) | collective-permute-done | bytes 229408 | tf_op jit(solution)/shard_map/ppermute | solution.py:38
  62.0 10.1 %fusion.8 = bf16[128,1024]{1,0:T(8,128)(2,1)S(1)} fusion(bf16[128,7168]{1,0:T(8,128)(2,1)S(1)} %constant_dynamic-update-slice_fusion, bf16[1,1024,7168]{2,1,0:T(8,128)(2,1)} %param.15), kind=kOutput, calls=%fused_computation.11 | convolution fusion | flops 1879179264 | bytes 16777216 | tf_op jit(solution)/shard_map/dot_general | solution.py:160
  72.1 1.6 collective-permute-start.5
  73.7 1.6 collective-permute-start.6
  75.4 9.7 %collective-permute-done.5 = bf16[32,7168]{1,0:T(8,128)(2,1)S(1)} collective-permute-done((bf16[32,7168]{1,0:T(8,128)(2,1)S(1)}, bf16[32,7168]{1,0:T(8,128)(2,1)S(1)}, u32[]{:S(2)}, u32[]{:S(2)}) %collective-permute-start.5) | collective-permute-done | bytes 458784 | tf_op jit(solution)/shard_map/ppermute | solution.py:38
  85.1 0.8 constant_dynamic-update-slice_fusion.159
  86.4 0.8 constant_dynamic-update-slice_fusion.158
  87.2 1.6 constant_dynamic-update-slice_fusion.144
  88.8 0.7 constant_dynamic-update-slice_fusion.143
  89.5 0.8 constant_dynamic-update-slice_fusion.142
  90.3 0.8 constant_dynamic-update-slice_fusion.141
  91.2 9.2 %collective-permute-start.12 = (bf16[48,7168]{1,0:T(8,128)(2,1)S(1)}, bf16[48,7168]{1,0:T(8,128)(2,1)S(1)}, u32[]{:S(2)}, u32[]{:S(2)}) collective-permute-start(bf16[48,7168]{1,0:T(8,128)(2,1)S(1)} %get-tuple-element.108), channel_id=1, source_target_pairs={{0,2},{1,3},{2,4},{3,5},{4,6},{5,7},{6,0},{7,1},{8,10},{9,11},{10,... | collective-permute-start | bytes 2064392 | tf_op jit(solution)/shard_map/ppermute | solution.py:38
  100.6 1.6 collective-permute-start.15
  102.2 1.0 collective-permute-start.16
  103.2 12.7 %collective-permute-done.11 = bf16[48,7168]{1,0:T(8,128)(2,1)S(1)} collective-permute-done((bf16[48,7168]{1,0:T(8,128)(2,1)S(1)}, bf16[48,7168]{1,0:T(8,128)(2,1)S(1)}, u32[]{:S(2)}, u32[]{:S(2)}) %collective-permute-start.11) | collective-permute-done | bytes 688160 | tf_op jit(solution)/shard_map/ppermute | solution.py:38
  115.9 1.2 constant_dynamic-update-slice_fusion.140
  117.1 15.1 %collective-permute-done.12 = bf16[48,7168]{1,0:T(8,128)(2,1)S(1)} collective-permute-done((bf16[48,7168]{1,0:T(8,128)(2,1)S(1)}, bf16[48,7168]{1,0:T(8,128)(2,1)S(1)}, u32[]{:S(2)}, u32[]{:S(2)}) %collective-permute-start.12) | collective-permute-done | bytes 688160 | tf_op jit(solution)/shard_map/ppermute | solution.py:38
  132.2 1.2 constant_dynamic-update-slice_fusion.139
  133.4 2.0 collective-permute-start.14
  135.4 1.4 pad_maximum_fusion
  136.8 11.3 %collective-permute-done.13 = bf16[24,7168]{1,0:T(8,128)(2,1)S(1)} collective-permute-done((bf16[24,7168]{1,0:T(8,128)(2,1)S(1)}, bf16[24,7168]{1,0:T(8,128)(2,1)S(1)}, u32[]{:S(2)}, u32[]{:S(2)}) %collective-permute-start.13) | collective-permute-done | bytes 344096 | tf_op jit(solution)/shard_map/ppermute | solution.py:38
  148.2 0.9 constant_dynamic-update-slice_fusion.138
  149.1 0.9 constant_dynamic-update-slice_fusion.137
  150.0 1.0 constant_dynamic-update-slice_fusion.149
  151.0 1.0 constant_dynamic-update-slice_fusion.148
  152.0 1.0 constant_dynamic-update-slice_fusion.147
  153.0 10.8 %fusion.11 = bf16[128,1024]{1,0:T(8,128)(2,1)S(1)} fusion(bf16[128,7168]{1,0:T(8,128)(2,1)S(1)} %collective-permute-done.4, bf16[1,1024,7168]{2,1,0:T(8,128)(2,1)} %param.15), kind=kOutput, calls=%fused_computation.12 | convolution fusion | flops 1879179264 | bytes 16777216 | tf_op jit(solution)/shard_map/dot_general | solution.py:160
  164.5 0.9 copy.66
  165.3 4.1 %all-to-all-start = ((bf16[8,32,1024]{2,1,0:T(8,128)(2,1)}), bf16[8,32,1024]{2,1,0:T(8,128)(2,1)}, u32[]{:S(2)}, u32[]{:S(2)}) async-start(bf16[8,32,1024]{2,1,0:T(8,128)(2,1)} %bitcast.645), calls=%async_computation | async-start | bytes 1048576 | tf_op jit(solution)/shard_map/all_to_all | solution.py:180
  172.1 0.7 copy-done.3
  172.9 1.0 fusion.26
  173.9 10.9 %all-to-all-done = bf16[8,32,1024]{2,1,0:T(8,128)(2,1)} async-done(((bf16[8,32,1024]{2,1,0:T(8,128)(2,1)}), bf16[8,32,1024]{2,1,0:T(8,128)(2,1)}, u32[]{:S(2)}, u32[]{:S(2)}) %all-to-all-start) | async-done | bytes 524320 | tf_op jit(solution)/shard_map/all_to_all | solution.py:180
  184.8 1.2 fusion.36
  186.0 1.5 multiply_convert_fusion
  187.5 3.5 %constant_dynamic-update-slice_fusion.146 = bf16[768,7168]{1,0:T(8,128)(2,1)} fusion(bf16[768,7168]{1,0:T(8,128)(2,1)} %constant_dynamic-update-slice_fusion.147, bf16[192,7168]{1,0:T(8,128)(2,1)} %collective-permute-done.18), kind=kLoop, calls=%fused_computation.199 | loop fusion | bytes 5505024
  191.1 2.9 %constant_dynamic-update-slice_fusion.145 = bf16[768,7168]{1,0:T(8,128)(2,1)} fusion(bf16[768,7168]{1,0:T(8,128)(2,1)} %constant_dynamic-update-slice_fusion.146, bf16[128,7168]{1,0:T(8,128)(2,1)} %collective-permute-done.19), kind=kLoop, calls=%fused_computation.198 | loop fusion | bytes 3670016 | tf_op jit(solution)/shard_map/concatenate | solution.py:194
  194.0 6.0 %fusion.42 = f32[256,7168]{1,0:T(8,128)S(1)} fusion(bf16[768,256]{1,0:T(8,128)(2,1)S(1)} %copy-done.4, bf16[768,7168]{1,0:T(8,128)(2,1)} %constant_dynamic-update-slice_fusion.145), kind=kOutput, calls=%fused_computation.392 | convolution fusion | flops 2818572288 | bytes 18743296 | tf_op jit(solution)/shard_map/dot_general | solution.py:192
  200.0 4.3 %fusion.4 = f32[1,256,7168]{2,1,0:T(8,128)} fusion(f32[256,7168]{1,0:T(8,128)S(1)} %fusion.42, bf16[256,256]{1,0:T(8,128)(2,1)S(1)} %copy-done.6, bf16[128,7168]{1,0:T(8,128)(2,1)S(1)} %copy-done.1, bf16[128,7168]{1,0:T(8,128)(2,1)S(1)} %constant_dynamic-update-slice_fusion), kind=kOutput, calls=%fused_computation.5 | convolution fusion | flops 948699136 | bytes 18481152 | tf_op jit(solution)/shard_map/dot_general | solution.py:192
  (188 shorter events, 6.3 us)
Async XLA Ops:
  0.6 35.5 %collective-permute-start = (bf16[32,7168]{1,0:T(8,128)(2,1)}, bf16[32,7168]{1,0:T(8,128)(2,1)}, u32[]{:S(2)}, u32[]{:S(2)}) collective-permute-start(bf16[32,7168]{1,0:T(8,128)(2,1)} %param.13), channel_id=1, source_target_pairs={{0,6},{1,7},{2,0},{3,1},{4,2},{5,3},{6,4},{7,5},{8,14},{9,15},{10,... | collective-permute-start | bytes 1376264 | tf_op jit(solution)/shard_map/ppermute | solution.py:38
  5.8 38.1 %collective-permute-start.1 = (bf16[32,7168]{1,0:T(8,128)(2,1)}, bf16[32,7168]{1,0:T(8,128)(2,1)}, u32[]{:S(2)}, u32[]{:S(2)}) collective-permute-start(bf16[32,7168]{1,0:T(8,128)(2,1)} %param.13), channel_id=1, source_target_pairs={{0,2},{1,3},{2,4},{3,5},{4,6},{5,7},{6,0},{7,1},{8,10},{9,11},{10,... | collective-permute-start | bytes 1376264 | tf_op jit(solution)/shard_map/ppermute | solution.py:38
  7.5 4.7 %copy-start.12 = (s32[32,4]{0,1:T(4,128)S(1)}, s32[32,4]{0,1:T(4,128)}, u32[]{:S(2)}) copy-start(s32[32,4]{0,1:T(4,128)} %param.9) | copy-start | bytes 1540
  7.5 4.7 %copy-start.13 = (s32[8]{0:T(128)S(1)}, s32[8]{0:T(128)}, u32[]{:S(2)}) copy-start(s32[8]{0:T(128)} %param.10) | copy-start | bytes 100
  7.6 4.8 %copy-start.11 = (bf16[32,256]{1,0:T(8,128)(2,1)S(1)}, bf16[32,256]{1,0:T(8,128)(2,1)}, u32[]{:S(2)}) copy-start(bf16[32,256]{1,0:T(8,128)(2,1)} %param.17) | copy-start | bytes 49156
  13.2 7.4 %copy-start.2 = (bf16[32,7168]{1,0:T(8,128)(2,1)S(1)}, bf16[32,7168]{1,0:T(8,128)(2,1)}, u32[]{:S(2)}) copy-start(bf16[32,7168]{1,0:T(8,128)(2,1)} %param.13) | copy-start | bytes 1376260
  14.6 150.7 %all-to-all-start.1 = ((bf16[32,32,736]{2,1,0:T(8,128)(2,1)}), bf16[32,32,736]{2,1,0:T(8,128)(2,1)S(1)}, u32[]{:S(2)}, u32[]{:S(2)}) async-start(bf16[32,32,736]{2,1,0:T(8,128)(2,1)} %pad_maximum_fusion.1), calls=%async_computation.1 | async-start | bytes 3145728 | tf_op jit(solution)/shard_map/all_to_all | solution.py:127
  21.4 11.4 %collective-permute-start.7 = (bf16[8,7168]{1,0:T(8,128)(2,1)}, bf16[8,7168]{1,0:T(8,128)(2,1)}, u32[]{:S(2)}, u32[]{:S(2)}) collective-permute-start(bf16[8,7168]{1,0:T(8,128)(2,1)} %get-tuple-element.93), channel_id=1, source_target_pairs={{0,8},{1,9},{2,10},{3,11},{4,12},{5,13},{6,14},{7,15},{8,0},{9,1},... | collective-permute-start | bytes 344072 | tf_op jit(solution)/shard_map/ppermute | solution.py:38
  23.1 11.5 %collective-permute-start.8 = (bf16[8,7168]{1,0:T(8,128)(2,1)}, bf16[8,7168]{1,0:T(8,128)(2,1)S(1)}, u32[]{:S(2)}, u32[]{:S(2)}) collective-permute-start(bf16[8,7168]{1,0:T(8,128)(2,1)} %get-tuple-element.92), channel_id=1, source_target_pairs={{0,16},{1,17},{2,18},{3,19},{4,20},{5,21},{6,22},{7,23},{8,24},{9,... | collective-permute-start | bytes 344072 | tf_op jit(solution)/shard_map/ppermute | solution.py:38
  33.8 55.8 %collective-permute-start.9 = (bf16[16,7168]{1,0:T(8,128)(2,1)S(1)}, bf16[16,7168]{1,0:T(8,128)(2,1)S(1)}, u32[]{:S(2)}, u32[]{:S(2)}) collective-permute-start(bf16[16,7168]{1,0:T(8,128)(2,1)S(1)} %pad_maximum_fusion.7), channel_id=1, source_target_pairs={{0,16},{1,17},{2,18},{3,19},{4,20},{5,21},{6,22},{7,23},{8,24},{9,... | collective-permute-start | bytes 688136 | tf_op jit(solution)/shard_map/ppermute | solution.py:38
  35.5 54.8 %collective-permute-start.10 = (bf16[16,7168]{1,0:T(8,128)(2,1)S(1)}, bf16[16,7168]{1,0:T(8,128)(2,1)S(1)}, u32[]{:S(2)}, u32[]{:S(2)}) collective-permute-start(bf16[16,7168]{1,0:T(8,128)(2,1)S(1)} %pad_maximum_fusion.8), channel_id=1, source_target_pairs={{0,8},{1,9},{2,10},{3,11},{4,12},{5,13},{6,14},{7,15},{8,0},{9,1},... | collective-permute-start | bytes 688136 | tf_op jit(solution)/shard_map/ppermute | solution.py:38
  37.1 19.9 %collective-permute-start.2 = (bf16[16,7168]{1,0:T(8,128)(2,1)S(1)}, bf16[16,7168]{1,0:T(8,128)(2,1)S(1)}, u32[]{:S(2)}, u32[]{:S(2)}) collective-permute-start(bf16[16,7168]{1,0:T(8,128)(2,1)S(1)} %slice.740), channel_id=1, source_target_pairs={{0,6},{1,7},{2,0},{3,1},{4,2},{5,3},{6,4},{7,5},{8,14},{9,15},{10,... | collective-permute-start | bytes 688136 | tf_op jit(solution)/shard_map/ppermute | solution.py:38
  44.8 17.0 %collective-permute-start.3 = (bf16[16,7168]{1,0:T(8,128)(2,1)S(1)}, bf16[16,7168]{1,0:T(8,128)(2,1)S(1)}, u32[]{:S(2)}, u32[]{:S(2)}) collective-permute-start(bf16[16,7168]{1,0:T(8,128)(2,1)S(1)} %slice.741), channel_id=1, source_target_pairs={{0,2},{1,3},{2,4},{3,5},{4,6},{5,7},{6,0},{7,1},{8,10},{9,11},{10,... | collective-permute-start | bytes 688136 | tf_op jit(solution)/shard_map/ppermute | solution.py:38
  61.8 91.2 %collective-permute-start.4 = (bf16[128,7168]{1,0:T(8,128)(2,1)S(1)}, bf16[128,7168]{1,0:T(8,128)(2,1)S(1)}, u32[]{:S(2)}, u32[]{:S(2)}) collective-permute-start(bf16[128,7168]{1,0:T(8,128)(2,1)S(1)} %constant_dynamic-update-slice_fusion), channel_id=1, source_target_pairs={{0,1},{1,0},{2,3},{3,2},{4,5},{5,4},{6,7},{7,6},{8,9},{9,8},{10,11... | collective-permute-start | bytes 5505032 | tf_op jit(solution)/shard_map/ppermute | solution.py:41
  72.1 13.0 %collective-permute-start.5 = (bf16[32,7168]{1,0:T(8,128)(2,1)S(1)}, bf16[32,7168]{1,0:T(8,128)(2,1)S(1)}, u32[]{:S(2)}, u32[]{:S(2)}) collective-permute-start(bf16[32,7168]{1,0:T(8,128)(2,1)S(1)} %pad_maximum_fusion.5), channel_id=1, source_target_pairs={{0,8},{1,9},{2,10},{3,11},{4,12},{5,13},{6,14},{7,15},{8,0},{9,1},... | collective-permute-start | bytes 1376264 | tf_op jit(solution)/shard_map/ppermute | solution.py:38
  73.7 12.7 %collective-permute-start.6 = (bf16[32,7168]{1,0:T(8,128)(2,1)S(1)}, bf16[32,7168]{1,0:T(8,128)(2,1)S(1)}, u32[]{:S(2)}, u32[]{:S(2)}) collective-permute-start(bf16[32,7168]{1,0:T(8,128)(2,1)S(1)} %pad_maximum_fusion.6), channel_id=1, source_target_pairs={{0,16},{1,17},{2,18},{3,19},{4,20},{5,21},{6,22},{7,23},{8,24},{9,... | collective-permute-start | bytes 1376264 | tf_op jit(solution)/shard_map/ppermute | solution.py:38
  91.2 24.7 %collective-permute-start.11 = (bf16[48,7168]{1,0:T(8,128)(2,1)S(1)}, bf16[48,7168]{1,0:T(8,128)(2,1)S(1)}, u32[]{:S(2)}, u32[]{:S(2)}) collective-permute-start(bf16[48,7168]{1,0:T(8,128)(2,1)S(1)} %get-tuple-element.108), channel_id=1, source_target_pairs={{0,6},{1,7},{2,0},{3,1},{4,2},{5,3},{6,4},{7,5},{8,14},{9,15},{10,... | collective-permute-start | bytes 2064392 | tf_op jit(solution)/shard_map/ppermute | solution.py:38
  91.2 41.0 %collective-permute-start.12 = (bf16[48,7168]{1,0:T(8,128)(2,1)S(1)}, bf16[48,7168]{1,0:T(8,128)(2,1)S(1)}, u32[]{:S(2)}, u32[]{:S(2)}) collective-permute-start(bf16[48,7168]{1,0:T(8,128)(2,1)S(1)} %get-tuple-element.108), channel_id=1, source_target_pairs={{0,2},{1,3},{2,4},{3,5},{4,6},{5,7},{6,0},{7,1},{8,10},{9,11},{10,... | collective-permute-start | bytes 2064392 | tf_op jit(solution)/shard_map/ppermute | solution.py:38
  100.6 32.8 %collective-permute-start.15 = (bf16[64,7168]{1,0:T(8,128)(2,1)S(1)}, bf16[64,7168]{1,0:T(8,128)(2,1)S(1)}, u32[]{:S(2)}, u32[]{:S(2)}) collective-permute-start(bf16[64,7168]{1,0:T(8,128)(2,1)S(1)} %get-tuple-element.90), channel_id=1, source_target_pairs={{0,16},{1,17},{2,18},{3,19},{4,20},{5,21},{6,22},{7,23},{8,24},{9,... | collective-permute-start | bytes 2752520 | tf_op jit(solution)/shard_map/ppermute | solution.py:38
  102.2 33.3 %collective-permute-start.16 = (bf16[64,7168]{1,0:T(8,128)(2,1)S(1)}, bf16[64,7168]{1,0:T(8,128)(2,1)S(1)}, u32[]{:S(2)}, u32[]{:S(2)}) collective-permute-start(bf16[64,7168]{1,0:T(8,128)(2,1)S(1)} %get-tuple-element.91), channel_id=1, source_target_pairs={{0,8},{1,9},{2,10},{3,11},{4,12},{5,13},{6,14},{7,15},{8,0},{9,1},... | collective-permute-start | bytes 2752520 | tf_op jit(solution)/shard_map/ppermute | solution.py:38
  115.9 36.2 %collective-permute-start.17 = (bf16[64,7168]{1,0:T(8,128)(2,1)S(1)}, bf16[64,7168]{1,0:T(8,128)(2,1)S(1)}, u32[]{:S(2)}, u32[]{:S(2)}) collective-permute-start(bf16[64,7168]{1,0:T(8,128)(2,1)S(1)} %get-tuple-element.89), channel_id=1, source_target_pairs={{0,1},{1,0},{2,3},{3,2},{4,5},{5,4},{6,7},{7,6},{8,9},{9,8},{10,11... | collective-permute-start | bytes 2752520 | tf_op jit(solution)/shard_map/ppermute | solution.py:41
  132.2 16.0 %collective-permute-start.13 = (bf16[24,7168]{1,0:T(8,128)(2,1)S(1)}, bf16[24,7168]{1,0:T(8,128)(2,1)S(1)}, u32[]{:S(2)}, u32[]{:S(2)}) collective-permute-start(bf16[24,7168]{1,0:T(8,128)(2,1)S(1)} %slice.902), channel_id=1, source_target_pairs={{0,6},{1,7},{2,0},{3,1},{4,2},{5,3},{6,4},{7,5},{8,14},{9,15},{10,... | collective-permute-start | bytes 1032200 | tf_op jit(solution)/shard_map/ppermute | solution.py:38
  133.4 15.7 %collective-permute-start.14 = (bf16[24,7168]{1,0:T(8,128)(2,1)S(1)}, bf16[24,7168]{1,0:T(8,128)(2,1)S(1)}, u32[]{:S(2)}, u32[]{:S(2)}) collective-permute-start(bf16[24,7168]{1,0:T(8,128)(2,1)S(1)} %slice.903), channel_id=1, source_target_pairs={{0,2},{1,3},{2,4},{3,5},{4,6},{5,7},{6,0},{7,1},{8,10},{9,11},{10,... | collective-permute-start | bytes 1032200 | tf_op jit(solution)/shard_map/ppermute | solution.py:38
  136.8 54.3 %collective-permute-start.19 = (bf16[128,7168]{1,0:T(8,128)(2,1)}, bf16[128,7168]{1,0:T(8,128)(2,1)}, u32[]{:S(2)}, u32[]{:S(2)}) collective-permute-start(bf16[128,7168]{1,0:T(8,128)(2,1)} %pad_maximum_fusion), channel_id=1, source_target_pairs={{0,1},{1,0},{2,3},{3,2},{4,5},{5,4},{6,7},{7,6},{8,9},{9,8},{10,11... | collective-permute-start | bytes 5505032 | tf_op jit(solution)/shard_map/ppermute | solution.py:41
  150.0 37.6 %collective-permute-start.18 = (bf16[192,7168]{1,0:T(8,128)(2,1)}, bf16[192,7168]{1,0:T(8,128)(2,1)}, u32[]{:S(2)}, u32[]{:S(2)}) collective-permute-start(bf16[192,7168]{1,0:T(8,128)(2,1)} %get-tuple-element.94), channel_id=1, source_target_pairs={{0,1},{1,0},{2,3},{3,2},{4,5},{5,4},{6,7},{7,6},{8,9},{9,8},{10,11... | collective-permute-start | bytes 8257544 | tf_op jit(solution)/shard_map/ppermute | solution.py:41
  153.0 10.8 %copy-start = (bf16[128,7168]{1,0:T(8,128)(2,1)}, bf16[128,7168]{1,0:T(8,128)(2,1)S(1)}, u32[]{:S(2)}) copy-start(bf16[128,7168]{1,0:T(8,128)(2,1)S(1)} %collective-permute-done.4) | copy-start | bytes 5505028
  165.3 19.5 %all-to-all-start = ((bf16[8,32,1024]{2,1,0:T(8,128)(2,1)}), bf16[8,32,1024]{2,1,0:T(8,128)(2,1)}, u32[]{:S(2)}, u32[]{:S(2)}) async-start(bf16[8,32,1024]{2,1,0:T(8,128)(2,1)} %bitcast.645), calls=%async_computation | async-start | bytes 1048576 | tf_op jit(solution)/shard_map/all_to_all | solution.py:180
  170.1 15.8 %copy-start.7 = (pred[1,32,4]{2,1,0:T(8,128)(4,1)S(1)}, pred[1,32,4]{2,1,0:T(8,128)(4,1)}, u32[]{:S(2)}) copy-start(pred[1,32,4]{2,1,0:T(8,128)(4,1)} %copy.77) | copy-start | bytes 388
  170.1 15.8 %copy-start.8 = (pred[1,32,4]{2,1,0:T(8,128)(4,1)S(1)}, pred[1,32,4]{2,1,0:T(8,128)(4,1)}, u32[]{:S(2)}) copy-start(pred[1,32,4]{2,1,0:T(8,128)(4,1)} %copy.76) | copy-start | bytes 388
  170.2 15.8 %copy-start.9 = (pred[1,32,4]{2,1,0:T(8,128)(4,1)S(1)}, pred[1,32,4]{2,1,0:T(8,128)(4,1)}, u32[]{:S(2)}) copy-start(pred[1,32,4]{2,1,0:T(8,128)(4,1)} %copy.75) | copy-start | bytes 388
  170.2 15.8 %copy-start.10 = (pred[1,32,4]{2,1,0:T(8,128)(4,1)S(1)}, pred[1,32,4]{2,1,0:T(8,128)(4,1)}, u32[]{:S(2)}) copy-start(pred[1,32,4]{2,1,0:T(8,128)(4,1)} %copy.74) | copy-start | bytes 388
  171.5 0.7 copy-start.5
  172.1 0.7 copy-start.3
  191.1 2.9 %copy-start.4 = (bf16[768,256]{1,0:T(8,128)(2,1)S(1)}, bf16[768,256]{1,0:T(8,128)(2,1)}, u32[]{:S(2)}) copy-start(bf16[768,256]{1,0:T(8,128)(2,1)} %copy-done.3) | copy-start | bytes 1179652
  194.0 6.0 %copy-start.1 = (bf16[128,7168]{1,0:T(8,128)(2,1)S(1)}, bf16[128,7168]{1,0:T(8,128)(2,1)}, u32[]{:S(2)}) copy-start(bf16[128,7168]{1,0:T(8,128)(2,1)} %copy-done) | copy-start | bytes 5505028
  194.0 6.0 %copy-start.6 = (bf16[256,256]{1,0:T(8,128)(2,1)S(1)}, bf16[256,256]{1,0:T(8,128)(2,1)}, u32[]{:S(2)}) copy-start(bf16[256,256]{1,0:T(8,128)(2,1)} %copy-done.5) | copy-start | bytes 393220
